TPU v7x, 128 devices: a whole 4x4x4 slice. The times are simulated.
128 devices in a mesh: row: 8 (over z, y_lo), col: 16 (over x, y_hi, core).
Axes of the slice: x: 4, y: 4 (y_hi: 2, y_lo: 2; y = y_hi * 2 + y_lo), z: 4, core: 2. Of those that a mesh axis runs over, the one named last changes fastest.
Arguments:
- right_side: float32 [512, 512, 512], P(('row', 'col')), may hold values from -51 to 51
- coupling: float32 [512, 512, 512], P(('row', 'col')), may hold values from 0.01 to 0.3
Outputs:
- solution: float32 [512, 512, 512], P(('row', 'col'))
- residual: float32 [512, 512, 512], P(('row', 'col'))
- residual_norm: float32 [1], replicated
All inputs are finite; a program needn't handle non-finite values.
Results may differ from a plain program's by a relative error of at most 0.0003.
Values sent between devices are 32-bit elements; how exact they have to be, the bound alone decides.
A program may use at most 128 MiB of HBM per device.

v0:
```python
import math

import jax
import jax.numpy as jnp
import numpy as np
from jax import lax
from jax.experimental import pallas as pl
from jax.experimental.pallas import tpu as pltpu
from jax.sharding import PartitionSpec as P

ROW_COL = ("row", "col")
MESH = pl.DeviceIdType.MESH
SIZE = 512
HALF = SIZE // 2
DEVICES = 128
OWN = SIZE // DEVICES
PLANES = OWN + 1
F32, BF16 = jnp.float32, jnp.bfloat16
EVEN, ODD, ODD_T = 0, 2, 4


def tables():
    n = np.arange(HALF)

    def cas(product):
        angle = 2.0 * math.pi * (product % SIZE) / SIZE
        return np.cos(angle) + np.sin(angle)

    parts = []
    even, odd = cas(n[:, None] * (2 * n)), cas(n[:, None] * (2 * n + 1))
    for table in (even, odd, odd.T):
        high = table.astype(BF16)
        parts += [high, (table - high.astype(np.float64)).astype(BF16)]
    return np.stack(parts)


def split(field):
    high = field.astype(BF16)
    return high, (field - high.astype(F32)).astype(BF16)


def times_right(field, tab, index):
    high, low = split(field)
    table_high, table_low = tab[index], tab[index + 1]
    return jnp.dot(
        jnp.concatenate([high, high, low], axis=1),
        jnp.concatenate([table_high, table_low, table_high], axis=0),
        preferred_element_type=F32,
    )


def times_left(tab, index, field):
    high, low = split(field)
    table_high, table_low = tab[index], tab[index + 1]
    return jnp.dot(
        jnp.concatenate([table_high, table_low, table_high], axis=1),
        jnp.concatenate([high, high, low], axis=0),
        preferred_element_type=F32,
    )


def wave(index):
    signed = jnp.where(2 * index < SIZE, index, index - SIZE).astype(F32)
    return jnp.square(signed * (2.0 * math.pi / SIZE))


def partner(me, i):
    core = me & 1
    sign = 1 - 2 * core
    y = (me & 2) | (me >> 4 & 1)
    x = ((me >> 2) + sign * i) & 3
    y = (y + sign * (i + (i >> 2))) & 3
    z = ((me >> 5) + sign * (i + (i >> 4))) & 3
    core = core ^ (i >> 6)
    return z * 2 + (y & 1), x * 4 + (y & 2) + core


def for_partners(me, act):
    def step(i, carry):
        row, col = partner(me, i)
        act(row, col, row * 16 + col)
        return carry

    lax.fori_loop(1, DEVICES, step, 0)


def kernel(
    rhs_hbm, coupling_hbm, tab_hbm,
    solution_ref, residual_ref, norm_ref,
    rhs, coupling, tab, send1, recv1, send2, recv2, part, field, sums,
    load_sem, plane_sem, own_sem, send_sem, recv_sem, pair_sem,
):
    row, col = lax.axis_index("row"), lax.axis_index("col")
    me = row * 16 + col
    core = me & 1
    load_tab = pltpu.make_async_copy(tab_hbm, tab, load_sem.at[0])
    load_coupling = pltpu.make_async_copy(coupling_hbm, coupling, load_sem.at[1])

    def load_plane(p):
        return pltpu.make_async_copy(rhs_hbm.at[p], rhs.at[p], plane_sem.at[p])

    load_tab.start()
    for p in range(OWN):
        load_plane(p).start()
    load_coupling.start()

    barrier = pltpu.get_barrier_semaphore()

    def greet(r, c, _):
        pl.semaphore_signal(barrier, inc=1, device_id=(r, c), device_id_type=MESH)

    for_partners(me, greet)

    def send(src, dst, stage, r, c):
        pltpu.make_async_remote_copy(
            src_ref=src,
            dst_ref=dst,
            send_sem=send_sem.at[stage],
            recv_sem=recv_sem.at[stage],
            device_id=(r, c),
            device_id_type=MESH,
        ).start()

    def wait_for(like, sem, stage):
        pltpu.make_async_copy(like, like, sem.at[stage]).wait()

    def rows(start, count):
        return pl.ds(pl.multiple_of(start, 8), count)

    row_mode = lax.broadcasted_iota(jnp.int32, (8, HALF), 0)
    lane_mode = lax.broadcasted_iota(jnp.int32, (8, HALF), 1)

    def forward(h):
        def plane(p, carry):
            if h == 0:
                load_plane(p).wait()
            low, high = rhs[p, :, :HALF], rhs[p, :, HALF:]
            if h == 0:
                both = low + high
                mean = jnp.sum(jnp.sum(both, axis=0, keepdims=True), axis=1, keepdims=True)
                mean = mean * (1.0 / SIZE**2)
                lines = times_right(both - 2.0 * mean, tab, EVEN)
            else:
                lines = times_right(low - high, tab, ODD)
            low, high = lines[:HALF], lines[HALF:]
            for side in range(2):
                if side == 0:
                    modes = times_left(tab, EVEN, low + high)
                    if h == 0:
                        constant = (row_mode == 0) & (lane_mode == 0)
                        top = modes[:8] + jnp.where(constant, mean * float(SIZE**2), 0.0)
                        modes = jnp.concatenate([top, modes[8:]], axis=0)
                else:
                    modes = times_left(tab, ODD_T, low - high)
                for g in range(32):
                    for q in range(2):
                        to = ((side * 32 + g) * 2 + q) * 8 * OWN
                        send1[h, rows(to + p * 8, 8)] = modes[
                            g * 8 : g * 8 + 8, q * 128 : q * 128 + 128
                        ]
            return carry

        lax.fori_loop(0, OWN, plane, 0)

    def send_forward(h):
        def piece(t):
            return send1.at[h, rows(t * 8 * OWN, 8 * OWN)]

        to = recv1.at[h, rows(me * 8 * OWN, 8 * OWN)]
        for_partners(me, lambda r, c, t: send(piece(t), to, h, r, c))
        pltpu.make_async_copy(piece(me), to, own_sem.at[h]).start()

    mode_z = lax.broadcasted_iota(jnp.int32, (HALF, 1), 0) * 2
    waves_z = (wave(mode_z), wave(mode_z + 1))
    lane = lax.broadcasted_iota(jnp.int32, (1, 128), 1)

    def along_z(h):
        wave_x = wave(2 * (me % 2 * 128 + lane) + h)

        def pair(i, carry):
            columns, wave_xy = [], []
            for b in range(2):
                columns.append(recv1[h, pl.ds(2 * i + b, SIZE, stride=8), :])
                order = lane * 0 + (me // 2 * 8 + 2 * i + b)
                mode_y = 2 * order - jnp.where(order < HALF, 0, SIZE - 1)
                wave_xy.append(wave(mode_y) + wave_x)
            lines = jnp.concatenate(columns, axis=1)
            wave_xy = jnp.concatenate(wave_xy, axis=1)
            total = jnp.sum(lines, axis=0, keepdims=True)
            lines = lines - total * (1.0 / SIZE)
            low, high = lines[:HALF], lines[HALF:]

            def scaled(spectrum, wave_z):
                eigen = wave_z + wave_xy
                positive = eigen > 0
                divisor = jnp.where(positive, eigen * float(SIZE**3), 1.0)
                inverse = 1.0 / divisor
                inverse = inverse * (2.0 - divisor * inverse)
                return jnp.where(positive, spectrum * inverse, 0.0)

            even = times_left(tab, EVEN, low + high)
            even = scaled(even + jnp.where(mode_z == 0, total, 0.0), waves_z[0])
            odd = scaled(times_left(tab, ODD_T, low - high), waves_z[1])
            even = times_left(tab, EVEN, even)
            odd = times_left(tab, ODD, odd)
            low, high = even + odd, even - odd
            for b in range(2):
                part_of = slice(b * 128, b * 128 + 128)
                at = 2 * i + b
                send2[h, pl.ds(at + 8, HALF, stride=8), :] = low[:, part_of]
                send2[h, pl.ds(at + 8 + 8 * HALF, HALF, stride=8), :] = high[:, part_of]
                send2[h, pl.ds(at, 1), :] = high[HALF - 1 :, part_of]
                send2[h, pl.ds(at + 8 + 8 * SIZE, 1), :] = low[:1, part_of]
            return carry

        lax.fori_loop(0, 4, pair, 0)

    def send_back(h):
        def piece(t):
            return send2.at[h, rows(t * 8 * OWN + t % 2 * 8, 8 * PLANES)]

        to = recv2.at[h, rows(me * 8 * PLANES, 8 * PLANES)]
        for_partners(me, lambda r, c, t: send(piece(t), to, 2 + h, r, c))
        pltpu.make_async_copy(piece(me), to, own_sem.at[2 + h]).start()

    def arrived(stage):
        if stage < 2:
            like, own = recv1.at[stage], 8 * OWN
        else:
            like, own = recv2.at[stage - 2], 8 * PLANES
        one = like.at[pl.ds(0, own)]
        pltpu.make_async_copy(one, one, own_sem.at[stage]).wait()
        most = like.at[pl.ds(0, (DEVICES - 1) * own)]
        pltpu.make_async_copy(most, most, recv_sem.at[stage]).wait()

    def sent(stage):
        like, own = (recv1, 8 * OWN) if stage < 2 else (recv2, 8 * PLANES)
        most = like.at[stage % 2, pl.ds(0, (DEVICES - 1) * own)]
        pltpu.make_async_copy(most, most, send_sem.at[stage]).wait()

    def inverse(h, j):
        columns = []
        for q in range(2):
            tiles = [
                recv2[h, rows((g * 2 + q) * 8 * PLANES + j * 8, 8)] for g in range(64)
            ]
            columns.append(jnp.concatenate(tiles, axis=0))
        modes = jnp.concatenate(columns, axis=1)
        even = times_left(tab, EVEN, modes[:HALF])
        odd = times_left(tab, ODD, modes[HALF:])
        lines = jnp.concatenate([even + odd, even - odd], axis=0)
        if h == 0:
            part[j] = times_right(lines, tab, EVEN)
        else:
            odd = times_right(lines, tab, ODD_T)
            even = part[j]
            field[j + core, :, :HALF] = even + odd
            field[j + core, :, HALF:] = even - odd

    load_tab.wait()
    forward(0)
    pl.semaphore_wait(barrier, DEVICES - 1)
    send_forward(0)
    forward(1)
    send_forward(1)
    arrived(0)
    along_z(0)
    arrived(1)
    send_back(0)
    along_z(1)
    send_back(1)

    arrived(2)

    def first_half(j, carry):
        inverse(0, j)
        return carry

    lax.fori_loop(0, PLANES, first_half, 0)
    arrived(3)
    swap = pltpu.make_async_remote_copy(
        src_ref=field.at[OWN - (OWN - 1) * core],
        dst_ref=field.at[(OWN + 1) * core],
        send_sem=pair_sem.at[0],
        recv_sem=pair_sem.at[1],
        device_id=(row, col + 1 - 2 * core),
        device_id_type=MESH,
    )
    turn = OWN * (1 - core)
    inverse(1, turn)
    swap.start()

    def second_half(k, carry):
        inverse(1, turn + (2 * core - 1) * k)
        return carry

    lax.fori_loop(1, PLANES, second_half, 0)
    swap.wait()
    load_coupling.wait()

    def finish(p, total):
        value = field[p + 1]
        lap = 6.0 * value - field[p] - field[p + 2]
        for axis in range(2):
            lap = lap - pltpu.roll(value, 1, axis) - pltpu.roll(value, SIZE - 1, axis)
        residual = rhs[p] - (coupling[p] * value + lap)
        solution_ref[p] = value
        residual_ref[p] = residual
        return total + jnp.sum(residual * residual, axis=0, keepdims=True)

    total = lax.fori_loop(0, OWN, finish, jnp.zeros((1, SIZE), F32))
    sums[me] = total[:, :128] + total[:, 128:256] + total[:, 256:384] + total[:, 384:]
    for_partners(me, lambda r, c, t: send(sums.at[me], sums.at[me], 4, r, c))
    for stage in range(4):
        sent(stage)
    most = sums.at[pl.ds(0, DEVICES - 1)]
    pltpu.make_async_copy(most, most, send_sem.at[4]).wait()
    pltpu.make_async_copy(most, most, recv_sem.at[4]).wait()
    norm_ref[...] = jnp.sqrt(jnp.sum(jnp.sum(sums[...], axis=0), axis=1, keepdims=True))


def shards(right_side, coupling):
    held = (OWN, SIZE, SIZE)
    dma = pltpu.SemaphoreType.DMA
    hbm = pl.BlockSpec(memory_space=pltpu.MemorySpace.HBM)
    vmem = pl.BlockSpec(memory_space=pltpu.VMEM)
    solution, residual, norm = pl.pallas_call(
        kernel,
        out_shape=(
            jax.ShapeDtypeStruct(held, F32),
            jax.ShapeDtypeStruct(held, F32),
            jax.ShapeDtypeStruct((1, 1), F32),
        ),
        in_specs=[hbm] * 3,
        out_specs=[vmem] * 3,
        scratch_shapes=[
            pltpu.VMEM(held, F32),
            pltpu.VMEM(held, F32),
            pltpu.VMEM((6, HALF, HALF), BF16),
            pltpu.VMEM((2, 8 * SIZE, 128), F32),
            pltpu.VMEM((2, 8 * SIZE, 128), F32),
            pltpu.VMEM((2, 8 * (SIZE + 2), 128), F32),
            pltpu.VMEM((2, 8 * PLANES * DEVICES, 128), F32),
            pltpu.VMEM((PLANES, SIZE, HALF), F32),
            pltpu.VMEM((OWN + 2, SIZE, SIZE), F32),
            pltpu.VMEM((DEVICES, 1, 128), F32),
            dma((2,)),
            dma((OWN,)),
            dma((4,)),
            dma((5,)),
            dma((5,)),
            dma((2,)),
        ],
        compiler_params=pltpu.CompilerParams(
            collective_id=0, has_side_effects=True, vmem_limit_bytes=44 * 2**20
        ),
    )(right_side, coupling, jnp.asarray(tables()))
    return solution, residual, norm.reshape(1)


def solution(mesh):
    placed = P(ROW_COL, None, None)
    return jax.shard_map(
        shards,
        mesh=mesh,
        in_specs=(placed, placed),
        out_specs=(placed, placed, P()),
        check_vma=False,
    )
```

profile of v0, /device:TPU:1, one launch (start us, length us, event | category | flops | bytes accessed | tf_op | source)
XLA Modules:
  0.0 148.6 jit_solution(7760509086446293023)
XLA Ops:
  0.6 0.0 copy-start
  0.6 1.1 copy-done
  1.8 141.0 %shard_map.58 = (f32[4,512,512]{2,1,0:T(8,128)S(1)}, f32[4,512,512]{2,1,0:T(8,128)S(1)}, f32[1,1]{1,0:T(1,128)}) custom-call(f32[4,512,512]{2,1,0:T(8,128)} %rhs_hbm.1, f32[4,512,512]{2,1,0:T(8,128)} %coupling_hbm.1, bf16[6,256,256]{2,1,0:T(8,128)(2,1)S(1)} %copy-done), custom_call_target="tpu_custom_call" | custom-call | tf_op jit(solution)/shard_map/pallas_call | solution.py:327
  142.8 2.0 %copy.9 = f32[4,512,512]{2,1,0:T(8,128)} copy(f32[4,512,512]{2,1,0:T(8,128)S(1)} %get-tuple-element.12) | data formatting | bytes 8388608
  144.8 2.0 %copy.10 = f32[4,512,512]{2,1,0:T(8,128)} copy(f32[4,512,512]{2,1,0:T(8,128)S(1)} %get-tuple-element.13) | data formatting | bytes 8388608
Async XLA Ops:
  0.6 1.1 copy-start
where the time goes:
time: 149 us
  Pallas kernels  141 us (95%)
  local copies, waits for them, and re-layouts  5.16 us (3%)
  between operations  2.41 us (2%)
    pallas_call x1, Pallas kernels, shards(): pl.pallas_call(kernel, out_shape=(jax.ShapeDtypeStruct(held, F32), jax.Sh...  141 us
    unnamed x4, local copies, waits for them, and re-layouts  5.16 us

commit v1 on v0

--- a/solution.py
+++ b/solution.py
@@ -16,7 +16,7 @@
 OWN = SIZE // DEVICES
 PLANES = OWN + 1
 F32, BF16 = jnp.float32, jnp.bfloat16
-EVEN, ODD, ODD_T = 0, 2, 4
+EVEN, ODD, ODD_T = 0, 3, 6
 
 
 def tables():
@@ -29,32 +29,39 @@
     parts = []
     even, odd = cas(n[:, None] * (2 * n)), cas(n[:, None] * (2 * n + 1))
     for table in (even, odd, odd.T):
-        high = table.astype(BF16)
-        parts += [high, (table - high.astype(np.float64)).astype(BF16)]
+        for _ in range(3):
+            parts.append(table.astype(BF16))
+            table = table - parts[-1].astype(np.float64)
     return np.stack(parts)
 
 
-def split(field):
-    high = field.astype(BF16)
-    return high, (field - high.astype(F32)).astype(BF16)
-
-
-def times_right(field, tab, index):
-    high, low = split(field)
-    table_high, table_low = tab[index], tab[index + 1]
+def split(field, terms):
+    parts = []
+    for term in range(terms):
+        parts.append(field.astype(BF16))
+        if term < terms - 1:
+            field = field - parts[-1].astype(F32)
+    return parts
+
+
+FORWARD = ((0, 0), (0, 1), (1, 0))
+INVERSE = ((0, 0), (0, 1), (0, 2), (1, 0), (1, 1), (2, 0))
+
+
+def times_right(field, tab, index, pairs):
+    parts = split(field, 2 if pairs is FORWARD else 3)
     return jnp.dot(
-        jnp.concatenate([high, high, low], axis=1),
-        jnp.concatenate([table_high, table_low, table_high], axis=0),
+        jnp.concatenate([parts[d] for d, _ in pairs], axis=1),
+        jnp.concatenate([tab[index + t] for _, t in pairs], axis=0),
         preferred_element_type=F32,
     )
 
 
-def times_left(tab, index, field):
-    high, low = split(field)
-    table_high, table_low = tab[index], tab[index + 1]
+def times_left(tab, index, field, pairs):
+    parts = split(field, 2 if pairs is FORWARD else 3)
     return jnp.dot(
-        jnp.concatenate([table_high, table_low, table_high], axis=1),
-        jnp.concatenate([high, high, low], axis=0),
+        jnp.concatenate([tab[index + t] for _, t in pairs], axis=1),
+        jnp.concatenate([parts[d] for d, _ in pairs], axis=0),
         preferred_element_type=F32,
     )
 
@@ -75,13 +82,30 @@
     return z * 2 + (y & 1), x * 4 + (y & 2) + core
 
 
-def for_partners(me, act):
-    def step(i, carry):
-        row, col = partner(me, i)
+def far_first(me, i):
+    def offset(k):
+        return (1 - (k & 1)) * 2 | ((k ^ (k >> 1)) & 1)
+
+    y = (me & 2) | (me >> 4 & 1)
+    z = ((me >> 5) + offset(i >> 5)) & 3
+    y = (y + offset(i >> 3 & 3)) & 3
+    x = ((me >> 2) + offset(i >> 1 & 3)) & 3
+    core = (me & 1) ^ 1 ^ (i & 1)
+    return z * 2 + (y & 1), x * 4 + (y & 2) + core
+
+
+def for_partners(me, act, order=partner, first=1):
+    def one(i):
+        row, col = order(me, i)
         act(row, col, row * 16 + col)
+
+    def three(k, carry):
+        for i in range(3):
+            one(first + 3 * k + i)
         return carry
 
-    lax.fori_loop(1, DEVICES, step, 0)
+    lax.fori_loop(0, 42, three, 0)
+    one(first + 126)
 
 
 def kernel(
@@ -102,14 +126,13 @@
     load_tab.start()
     for p in range(OWN):
         load_plane(p).start()
-    load_coupling.start()
 
     barrier = pltpu.get_barrier_semaphore()
 
     def greet(r, c, _):
         pl.semaphore_signal(barrier, inc=1, device_id=(r, c), device_id_type=MESH)
 
-    for_partners(me, greet)
+    for_partners(me, greet, far_first, 0)
 
     def send(src, dst, stage, r, c):
         pltpu.make_async_remote_copy(
@@ -121,9 +144,6 @@
             device_id_type=MESH,
         ).start()
 
-    def wait_for(like, sem, stage):
-        pltpu.make_async_copy(like, like, sem.at[stage]).wait()
-
     def rows(start, count):
         return pl.ds(pl.multiple_of(start, 8), count)
 
@@ -139,19 +159,19 @@
                 both = low + high
                 mean = jnp.sum(jnp.sum(both, axis=0, keepdims=True), axis=1, keepdims=True)
                 mean = mean * (1.0 / SIZE**2)
-                lines = times_right(both - 2.0 * mean, tab, EVEN)
+                lines = times_right(both - 2.0 * mean, tab, EVEN, FORWARD)
             else:
-                lines = times_right(low - high, tab, ODD)
+                lines = times_right(low - high, tab, ODD, FORWARD)
             low, high = lines[:HALF], lines[HALF:]
             for side in range(2):
                 if side == 0:
-                    modes = times_left(tab, EVEN, low + high)
+                    modes = times_left(tab, EVEN, low + high, FORWARD)
                     if h == 0:
                         constant = (row_mode == 0) & (lane_mode == 0)
                         top = modes[:8] + jnp.where(constant, mean * float(SIZE**2), 0.0)
                         modes = jnp.concatenate([top, modes[8:]], axis=0)
                 else:
-                    modes = times_left(tab, ODD_T, low - high)
+                    modes = times_left(tab, ODD_T, low - high, FORWARD)
                 for g in range(32):
                     for q in range(2):
                         to = ((side * 32 + g) * 2 + q) * 8 * OWN
@@ -198,11 +218,11 @@
                 inverse = inverse * (2.0 - divisor * inverse)
                 return jnp.where(positive, spectrum * inverse, 0.0)
 
-            even = times_left(tab, EVEN, low + high)
+            even = times_left(tab, EVEN, low + high, FORWARD)
             even = scaled(even + jnp.where(mode_z == 0, total, 0.0), waves_z[0])
-            odd = scaled(times_left(tab, ODD_T, low - high), waves_z[1])
-            even = times_left(tab, EVEN, even)
-            odd = times_left(tab, ODD, odd)
+            odd = scaled(times_left(tab, ODD_T, low - high, FORWARD), waves_z[1])
+            even = times_left(tab, EVEN, even, INVERSE)
+            odd = times_left(tab, ODD, odd, INVERSE)
             low, high = even + odd, even - odd
             for b in range(2):
                 part_of = slice(b * 128, b * 128 + 128)
@@ -215,27 +235,36 @@
 
         lax.fori_loop(0, 4, pair, 0)
 
-    def send_back(h):
-        def piece(t):
-            return send2.at[h, rows(t * 8 * OWN + t % 2 * 8, 8 * PLANES)]
-
-        to = recv2.at[h, rows(me * 8 * PLANES, 8 * PLANES)]
-        for_partners(me, lambda r, c, t: send(piece(t), to, 2 + h, r, c))
-        pltpu.make_async_copy(piece(me), to, own_sem.at[2 + h]).start()
+    def group(stage, t):
+        side = t & 1
+        return {2: (0, 5), 3: (1 - side, 2), 4: (3 - side, 2), 5: (4 * side, 1)}[stage]
+
+    def send_back(stage):
+        h = 0 if stage == 2 else 1
+
+        def ends(t):
+            j, count = group(stage, t)
+            src = send2.at[h, rows((t * OWN + (t & 1) + j) * 8, 8 * count)]
+            return src, recv2.at[h, rows((me * PLANES + j) * 8, 8 * count)]
+
+        for_partners(me, lambda r, c, t: send(*ends(t), stage, r, c))
+        pltpu.make_async_copy(*ends(me), own_sem.at[stage]).start()
+
+    def bytes_of(stage):
+        if stage < 2:
+            return recv1.at[stage], 8 * OWN
+        return recv2.at[min(stage - 2, 1)], 8 * group(stage, 0)[1]
 
     def arrived(stage):
-        if stage < 2:
-            like, own = recv1.at[stage], 8 * OWN
-        else:
-            like, own = recv2.at[stage - 2], 8 * PLANES
+        like, own = bytes_of(stage)
         one = like.at[pl.ds(0, own)]
         pltpu.make_async_copy(one, one, own_sem.at[stage]).wait()
         most = like.at[pl.ds(0, (DEVICES - 1) * own)]
         pltpu.make_async_copy(most, most, recv_sem.at[stage]).wait()
 
     def sent(stage):
-        like, own = (recv1, 8 * OWN) if stage < 2 else (recv2, 8 * PLANES)
-        most = like.at[stage % 2, pl.ds(0, (DEVICES - 1) * own)]
+        like, own = bytes_of(stage)
+        most = like.at[pl.ds(0, (DEVICES - 1) * own)]
         pltpu.make_async_copy(most, most, send_sem.at[stage]).wait()
 
     def inverse(h, j):
@@ -246,13 +275,13 @@
             ]
             columns.append(jnp.concatenate(tiles, axis=0))
         modes = jnp.concatenate(columns, axis=1)
-        even = times_left(tab, EVEN, modes[:HALF])
-        odd = times_left(tab, ODD, modes[HALF:])
+        even = times_left(tab, EVEN, modes[:HALF], INVERSE)
+        odd = times_left(tab, ODD, modes[HALF:], INVERSE)
         lines = jnp.concatenate([even + odd, even - odd], axis=0)
         if h == 0:
-            part[j] = times_right(lines, tab, EVEN)
+            part[j] = times_right(lines, tab, EVEN, INVERSE)
         else:
-            odd = times_right(lines, tab, ODD_T)
+            odd = times_right(lines, tab, ODD_T, INVERSE)
             even = part[j]
             field[j + core, :, :HALF] = even + odd
             field[j + core, :, HALF:] = even - odd
@@ -261,14 +290,17 @@
     forward(0)
     pl.semaphore_wait(barrier, DEVICES - 1)
     send_forward(0)
+    load_coupling.start()
     forward(1)
     send_forward(1)
     arrived(0)
     along_z(0)
+    sent(1)
+    send_back(2)
     arrived(1)
-    send_back(0)
     along_z(1)
-    send_back(1)
+    for stage in (3, 4, 5):
+        send_back(stage)
 
     arrived(2)
 
@@ -277,7 +309,37 @@
         return carry
 
     lax.fori_loop(0, PLANES, first_half, 0)
+    def second_half(j, carry):
+        inverse(1, j)
+        return carry
+
+    BLOCK = 64
+    row_in = lax.broadcasted_iota(jnp.int32, (8, SIZE), 0)
+
+    def finish(p, total):
+        def block(k, total):
+            start = k * BLOCK
+            here = rows(start, BLOCK)
+            value = field[p + 1, here]
+            before = field[p + 1, pl.ds((start + SIZE - 1) & (SIZE - 1), 1)]
+            after = field[p + 1, pl.ds((start + BLOCK) & (SIZE - 1), 1)]
+            up = pltpu.roll(value, 1, 0)
+            up = jnp.concatenate([jnp.where(row_in == 0, before, up[:8]), up[8:]], axis=0)
+            down = pltpu.roll(value, BLOCK - 1, 0)
+            down = jnp.concatenate([down[:-8], jnp.where(row_in == 7, after, down[-8:])], axis=0)
+            lap = 6.0 * value - field[p, here] - field[p + 2, here] - up - down
+            lap = lap - pltpu.roll(value, 1, 1) - pltpu.roll(value, SIZE - 1, 1)
+            residual = rhs[p, here] - (coupling[p, here] * value + lap)
+            solution_ref[p, here] = value
+            residual_ref[p, here] = residual
+            return total + jnp.sum((residual * residual).reshape(BLOCK // 8, 8, SIZE), axis=0)
+
+        return lax.fori_loop(0, SIZE // BLOCK, block, total)
+
     arrived(3)
+    lax.fori_loop(1 - core, 3 - core, second_half, 0)
+    arrived(4)
+    lax.fori_loop(3 - core, 5 - core, second_half, 0)
     swap = pltpu.make_async_remote_copy(
         src_ref=field.at[OWN - (OWN - 1) * core],
         dst_ref=field.at[(OWN + 1) * core],
@@ -286,36 +348,22 @@
         device_id=(row, col + 1 - 2 * core),
         device_id_type=MESH,
     )
-    turn = OWN * (1 - core)
-    inverse(1, turn)
     swap.start()
-
-    def second_half(k, carry):
-        inverse(1, turn + (2 * core - 1) * k)
-        return carry
-
-    lax.fori_loop(1, PLANES, second_half, 0)
+    load_coupling.wait()
+    total = lax.fori_loop(1, OWN - 1, finish, jnp.zeros((8, SIZE), F32))
     swap.wait()
-    load_coupling.wait()
-
-    def finish(p, total):
-        value = field[p + 1]
-        lap = 6.0 * value - field[p] - field[p + 2]
-        for axis in range(2):
-            lap = lap - pltpu.roll(value, 1, axis) - pltpu.roll(value, SIZE - 1, axis)
-        residual = rhs[p] - (coupling[p] * value + lap)
-        solution_ref[p] = value
-        residual_ref[p] = residual
-        return total + jnp.sum(residual * residual, axis=0, keepdims=True)
-
-    total = lax.fori_loop(0, OWN, finish, jnp.zeros((1, SIZE), F32))
+    total = finish((OWN - 1) * (1 - core), total)
+    arrived(5)
+    inverse(1, OWN * core)
+    total = finish((OWN - 1) * core, total)
+    total = jnp.sum(total, axis=0, keepdims=True)
     sums[me] = total[:, :128] + total[:, 128:256] + total[:, 256:384] + total[:, 384:]
-    for_partners(me, lambda r, c, t: send(sums.at[me], sums.at[me], 4, r, c))
-    for stage in range(4):
+    for_partners(me, lambda r, c, t: send(sums.at[me], sums.at[me], 6, r, c), far_first, 0)
+    for stage in (0, 2, 3, 4, 5):
         sent(stage)
     most = sums.at[pl.ds(0, DEVICES - 1)]
-    pltpu.make_async_copy(most, most, send_sem.at[4]).wait()
-    pltpu.make_async_copy(most, most, recv_sem.at[4]).wait()
+    pltpu.make_async_copy(most, most, send_sem.at[6]).wait()
+    pltpu.make_async_copy(most, most, recv_sem.at[6]).wait()
     norm_ref[...] = jnp.sqrt(jnp.sum(jnp.sum(sums[...], axis=0), axis=1, keepdims=True))
 
 
@@ -336,7 +384,7 @@
         scratch_shapes=[
             pltpu.VMEM(held, F32),
             pltpu.VMEM(held, F32),
-            pltpu.VMEM((6, HALF, HALF), BF16),
+            pltpu.VMEM((9, HALF, HALF), BF16),
             pltpu.VMEM((2, 8 * SIZE, 128), F32),
             pltpu.VMEM((2, 8 * SIZE, 128), F32),
             pltpu.VMEM((2, 8 * (SIZE + 2), 128), F32),
@@ -346,9 +394,9 @@
             pltpu.VMEM((DEVICES, 1, 128), F32),
             dma((2,)),
             dma((OWN,)),
-            dma((4,)),
-            dma((5,)),
-            dma((5,)),
+            dma((6,)),
+            dma((7,)),
+            dma((7,)),
             dma((2,)),
         ],
         compiler_params=pltpu.CompilerParams(

time: 149 us -> 141 us (0.946)
  Pallas kernels: 141 us -> 133 us
    pallas_call x1, Pallas kernels: 141 us -> 133 us  [shards(): pl.pallas_call(kernel, out_shape=(jax.ShapeDtypeStruct(held, F32), jax.Sh...]
where the time goes in v1:
time: 141 us
  Pallas kernels  133 us (94%)
  local copies, waits for them, and re-layouts  5.29 us (4%)
  between operations  2.41 us (2%)
    pallas_call x1, Pallas kernels, shards(): pl.pallas_call(kernel, out_shape=(jax.ShapeDtypeStruct(held, F32), jax.Sh...  133 us
    unnamed x4, local copies, waits for them, and re-layouts  5.29 us

profile of v1, /device:TPU:1, one launch (start us, length us, event | category | flops | bytes accessed | tf_op | source)
XLA Modules:
  0.0 141.0 jit_solution(15741529260854926929)
XLA Ops:
  0.6 0.0 copy-start
  0.6 1.3 copy-done
  1.9 133.3 %shard_map.58 = (f32[4,512,512]{2,1,0:T(8,128)S(1)}, f32[4,512,512]{2,1,0:T(8,128)S(1)}, f32[1,1]{1,0:T(1,128)}) custom-call(f32[4,512,512]{2,1,0:T(8,128)} %rhs_hbm.1, f32[4,512,512]{2,1,0:T(8,128)} %coupling_hbm.1, bf16[9,256,256]{2,1,0:T(8,128)(2,1)S(1)} %copy-done), custom_call_target="tpu_custom_call" | custom-call | tf_op jit(solution)/shard_map/pallas_call | solution.py:375
  135.2 2.0 %copy.9 = f32[4,512,512]{2,1,0:T(8,128)} copy(f32[4,512,512]{2,1,0:T(8,128)S(1)} %get-tuple-element.12) | data formatting | bytes 8388608
  137.2 2.0 %copy.10 = f32[4,512,512]{2,1,0:T(8,128)} copy(f32[4,512,512]{2,1,0:T(8,128)S(1)} %get-tuple-element.13) | data formatting | bytes 8388608
Async XLA Ops:
  0.6 1.3 copy-start

commit v2 on v1

--- a/solution.py
+++ b/solution.py
@@ -74,8 +74,9 @@
 def partner(me, i):
     core = me & 1
     sign = 1 - 2 * core
+    i = i * 37 & 127
     y = (me & 2) | (me >> 4 & 1)
-    x = ((me >> 2) + sign * i) & 3
+    x = ((me >> 2) + sign * (i)) & 3
     y = (y + sign * (i + (i >> 2))) & 3
     z = ((me >> 5) + sign * (i + (i >> 4))) & 3
     core = core ^ (i >> 6)

time: 141 us -> 138 us (0.979)
  Pallas kernels: 133 us -> 130 us
    pallas_call x1, Pallas kernels: 133 us -> 130 us  [shards(): pl.pallas_call(kernel, out_shape=(jax.ShapeDtypeStruct(held, F32), jax.Sh...]
where the time goes in v2:
time: 138 us
  Pallas kernels  130 us (94%)
  local copies, waits for them, and re-layouts  5.29 us (4%)
  between operations  2.41 us (2%)
    pallas_call x1, Pallas kernels, shards(): pl.pallas_call(kernel, out_shape=(jax.ShapeDtypeStruct(held, F32), jax.Sh...  130 us
    unnamed x4, local copies, waits for them, and re-layouts  5.29 us

profile of v2, /device:TPU:1, one launch (start us, length us, event | category | flops | bytes accessed | tf_op | source)
XLA Modules:
  0.0 138.0 jit_solution(4539155452982018728)
XLA Ops:
  0.6 0.0 copy-start
  0.6 1.3 copy-done
  1.9 130.3 %shard_map.58 = (f32[4,512,512]{2,1,0:T(8,128)S(1)}, f32[4,512,512]{2,1,0:T(8,128)S(1)}, f32[1,1]{1,0:T(1,128)}) custom-call(f32[4,512,512]{2,1,0:T(8,128)} %rhs_hbm.1, f32[4,512,512]{2,1,0:T(8,128)} %coupling_hbm.1, bf16[9,256,256]{2,1,0:T(8,128)(2,1)S(1)} %copy-done), custom_call_target="tpu_custom_call" | custom-call | tf_op jit(solution)/shard_map/pallas_call | solution.py:376
  132.2 2.0 %copy.9 = f32[4,512,512]{2,1,0:T(8,128)} copy(f32[4,512,512]{2,1,0:T(8,128)S(1)} %get-tuple-element.12) | data formatting | bytes 8388608
  134.3 2.0 %copy.10 = f32[4,512,512]{2,1,0:T(8,128)} copy(f32[4,512,512]{2,1,0:T(8,128)S(1)} %get-tuple-element.13) | data formatting | bytes 8388608
Async XLA Ops:
  0.6 1.3 copy-start

commit v3 on v2

--- a/solution.py
+++ b/solution.py
@@ -151,7 +151,7 @@
     row_mode = lax.broadcasted_iota(jnp.int32, (8, HALF), 0)
     lane_mode = lax.broadcasted_iota(jnp.int32, (8, HALF), 1)
 
-    def forward(h):
+    def forward(h, first, last):
         def plane(p, carry):
             if h == 0:
                 load_plane(p).wait()
@@ -181,15 +181,17 @@
                         ]
             return carry
 
-        lax.fori_loop(0, OWN, plane, 0)
-
-    def send_forward(h):
-        def piece(t):
-            return send1.at[h, rows(t * 8 * OWN, 8 * OWN)]
-
-        to = recv1.at[h, rows(me * 8 * OWN, 8 * OWN)]
-        for_partners(me, lambda r, c, t: send(piece(t), to, h, r, c))
-        pltpu.make_async_copy(piece(me), to, own_sem.at[h]).start()
+        lax.fori_loop(first, last, plane, 0)
+
+    def send_forward(h, first, last):
+        def at(device):
+            return h, rows((device * OWN + first) * 8, 8 * (last - first))
+
+        to = recv1.at[at(me)]
+        for_partners(me, lambda r, c, t: send(send1.at[at(t)], to, h, r, c))
+        if last == OWN:
+            whole = rows(me * OWN * 8, 8 * OWN)
+            pltpu.make_async_copy(send1.at[h, whole], recv1.at[h, whole], own_sem.at[h]).start()
 
     mode_z = lax.broadcasted_iota(jnp.int32, (HALF, 1), 0) * 2
     waves_z = (wave(mode_z), wave(mode_z + 1))
@@ -288,12 +290,14 @@
             field[j + core, :, HALF:] = even - odd
 
     load_tab.wait()
-    forward(0)
+    forward(0, 0, 2)
     pl.semaphore_wait(barrier, DEVICES - 1)
-    send_forward(0)
+    send_forward(0, 0, 2)
+    forward(0, 2, OWN)
+    send_forward(0, 2, OWN)
     load_coupling.start()
-    forward(1)
-    send_forward(1)
+    forward(1, 0, OWN)
+    send_forward(1, 0, OWN)
     arrived(0)
     along_z(0)
     sent(1)

time: 138 us -> 136 us (0.986)
  Pallas kernels: 130 us -> 128 us
    pallas_call x1, Pallas kernels: 130 us -> 128 us  [shards(): pl.pallas_call(kernel, out_shape=(jax.ShapeDtypeStruct(held, F32), jax.Sh...]
where the time goes in v3:
time: 136 us
  Pallas kernels  128 us (94%)
  local copies, waits for them, and re-layouts  5.29 us (4%)
  between operations  2.41 us (2%)
    pallas_call x1, Pallas kernels, shards(): pl.pallas_call(kernel, out_shape=(jax.ShapeDtypeStruct(held, F32), jax.Sh...  128 us
    unnamed x4, local copies, waits for them, and re-layouts  5.29 us

profile of v3, /device:TPU:1, one launch (start us, length us, event | category | flops | bytes accessed | tf_op | source)
XLA Modules:
  0.0 136.1 jit_solution(6453655928711248399)
XLA Ops:
  0.6 0.0 copy-start
  0.6 1.3 copy-done
  1.9 128.4 %shard_map.58 = (f32[4,512,512]{2,1,0:T(8,128)S(1)}, f32[4,512,512]{2,1,0:T(8,128)S(1)}, f32[1,1]{1,0:T(1,128)}) custom-call(f32[4,512,512]{2,1,0:T(8,128)} %rhs_hbm.1, f32[4,512,512]{2,1,0:T(8,128)} %coupling_hbm.1, bf16[9,256,256]{2,1,0:T(8,128)(2,1)S(1)} %copy-done), custom_call_target="tpu_custom_call" | custom-call | tf_op jit(solution)/shard_map/pallas_call | solution.py:380
  130.3 2.0 %copy.9 = f32[4,512,512]{2,1,0:T(8,128)} copy(f32[4,512,512]{2,1,0:T(8,128)S(1)} %get-tuple-element.12) | data formatting | bytes 8388608
  132.4 2.0 %copy.10 = f32[4,512,512]{2,1,0:T(8,128)} copy(f32[4,512,512]{2,1,0:T(8,128)S(1)} %get-tuple-element.13) | data formatting | bytes 8388608
Async XLA Ops:
  0.6 1.3 copy-start
